TPU v7x, 128 devices: a whole 4x4x4 slice. The times are simulated.
128 devices in a mesh: expert: 16 (over y, x), mp: 8 (over z, core).
Axes of the slice: x: 4, y: 4, z: 4, core: 2. Of those that a mesh axis runs over, the one named last changes fastest.
Arguments:
- tokens: bfloat16 [2048, 7168], P('expert', 'mp'), may hold values from -0.625 to 0.625
- cotangent: bfloat16 [2048, 8, 2048], P('expert', None, 'mp'), may hold values from -3 to 3
- weights: bfloat16 [32, 7168, 2048], P('expert', 'mp'), may hold values from -0.0625 to 0.0625
- steps: float32 [32, 2048], P('expert', 'mp'), may hold values from 0.002 to 0.02
- expert_ids: int32 [2048, 8], P('expert'), may hold values from 0 to 31, all different within a row; in each aligned block of 128 rows (0 to 127, 128 to 255, ...) at most 64 rows name the same one
Outputs:
- token_grads: bfloat16 [2048, 7168], P('expert', 'mp')
- weight_grads: bfloat16 [32, 7168, 2048], P('expert', 'mp')
- step_grads: float32 [32, 2048], P('expert', 'mp')
Inputs may be any that keep to these rules, and one draw needn't show every extreme that they name: `expert_ids`: each row names 8 different experts; among the 128 rows of one index of the expert axis, no expert is named by more than 64 rows, a bound that some block reaches of them.
All inputs are finite; a program needn't handle non-finite values.
Results may differ from a plain program's by a relative error of at most 0.0058.
Values may be sent and summed in bfloat16 or wider, within the bound.
A program may use at most 128 MiB of HBM per device.

v0:
```python
import math
import jax
import jax.numpy as jnp
from jax import lax
from jax.sharding import PartitionSpec as P

qmax = 7.0
wiggle = 0.9
two_pi = 6.283185307179586


def quantize(weight_f, step_f):
    scaled = weight_f / step_f
    squash = jnp.tanh(scaled / qmax)
    clipped = qmax * squash
    angles = two_pi * clipped
    stair = clipped - wiggle * jnp.sin(angles) / two_pi
    slopes = (1.0 - wiggle * jnp.cos(angles)) * (1.0 - squash * squash)
    return (step_f * stair, slopes, stair - scaled * slopes)


def slot_table(routes_flat, experts, capacity):
    one_hot = (routes_flat[:, None] == jnp.arange(experts, dtype=jnp.int32)[None, :]).astype(
        jnp.int32
    )
    before = jnp.cumsum(one_hot, axis=0) - one_hot
    position = jnp.sum(before * one_hot, axis=1)
    slot_of = routes_flat * capacity + position
    route_count = routes_flat.shape[0]
    source_of = jnp.full((experts * capacity,), route_count, jnp.int32)
    source_of = source_of.at[slot_of].set(jnp.arange(route_count, dtype=jnp.int32))
    return (slot_of, source_of)


def per_device(tokens, cotangent, weights, steps, expert_ids):
    groups = lax.axis_size("expert")
    local_experts = weights.shape[0]
    experts = groups * local_experts
    tok_rows, top_k = expert_ids.shape
    capacity = tok_rows // 2
    width_part = tokens.shape[1]
    slot_of, source_of = slot_table(expert_ids.reshape(-1), experts, capacity)
    token_of = source_of // top_k
    padded_x = jnp.concatenate([tokens, jnp.zeros((1, width_part), tokens.dtype)], axis=0)
    x_slots = padded_x[token_of].reshape(groups, local_experts, capacity, width_part)
    full_steps = lax.all_gather(steps, "mp", axis=1, tiled=True)
    levels, slopes, step_slopes = quantize(weights.astype(jnp.float32), full_steps[:, None, :])
    quantized = levels.astype(jnp.bfloat16)
    part_width = cotangent.shape[2]
    padded_g = jnp.concatenate(
        [
            cotangent.reshape(tok_rows * top_k, part_width),
            jnp.zeros((1, part_width), cotangent.dtype),
        ],
        axis=0,
    )
    g_slots = padded_g[source_of].reshape(groups, local_experts, capacity, part_width)
    x_recv, g_part = (
        lax.all_to_all(x_slots, "expert", split_axis=0, concat_axis=0, tiled=True),
        lax.all_to_all(g_slots, "expert", split_axis=0, concat_axis=0, tiled=True),
    )
    g_recv = lax.all_gather(g_part, "mp", axis=3, tiled=True)
    raw = jnp.einsum("sjcd,sjcf->jdf", x_recv, g_recv, preferred_element_type=jnp.float32)
    weight_out = (raw * slopes).astype(jnp.bfloat16)
    full_width = width_part * lax.axis_size("mp")
    partial_steps = jnp.sum(raw * step_slopes, axis=1)
    step_out = lax.psum_scatter(partial_steps, "mp", scatter_dimension=1, tiled=True) * (
        1.0 / math.sqrt(full_width * qmax)
    )
    back_slots = jnp.einsum(
        "sjcf,jdf->sjcd", g_recv, quantized, preferred_element_type=jnp.float32
    ).astype(jnp.bfloat16)
    returned = lax.all_to_all(back_slots, "expert", split_axis=0, concat_axis=0, tiled=True)
    per_route = returned.reshape(experts * capacity, width_part)[slot_of]
    token_out = (
        per_route.reshape(tok_rows, top_k, width_part)
        .astype(jnp.float32)
        .sum(axis=1)
        .astype(jnp.bfloat16)
    )
    return (token_out, weight_out, step_out)


def solution(mesh):
    return jax.shard_map(
        per_device,
        mesh=mesh,
        in_specs=(
            P("expert", "mp"),
            P("expert", None, "mp"),
            P("expert", "mp", None),
            P("expert", "mp"),
            P("expert", None),
        ),
        out_specs=(P("expert", "mp"), P("expert", "mp", None), P("expert", "mp")),
        check_vma=False,
    )
```

profile of v0, /device:TPU:0, one launch (start us, length us, event | category | flops | bytes accessed | tf_op | source)
XLA Modules:
  0.0 306.8 jit_solution(9049717152482495890)
XLA Ops:
  7.2 0.8 copy.17
  8.2 0.7 broadcast_multiply_fusion
  8.9 9.0 %reduce-window.6 = s32[32,8,128]{2,1,0:T(8,128)S(1)} reduce-window(s32[32,8,128]{2,1,0:T(8,128)S(1)} %fusion.17, s32[]{:T(128)} %constant.43.clone.1), window={size=1x1x128 pad=0_0x0_0x127_0}, to_apply=%region_0.0 | reduce-window | flops 4161536 | bytes 262148 | tf_op jit(solution)/shard_map/reduce-window
  18.0 0.1 copy.19
  18.6 4.3 %scatter_custom_fusion = s32[2048]{0:T(1024)S(1)} fusion(s32[1024]{0:T(1024)S(1)} %bitcast.58, s32[1024]{0:T(1024)S(1)} %iota.11, s32[]{:T(128)} %constant.41.clone.1), kind=kCustom, calls=%fused_computation.44 | custom fusion | bytes 8196 | tf_op jit(solution)/shard_map/scatter | solution.py:31
  23.0 1.1 concatenate.6
  24.1 7.5 %gather_fusion = bf16[2048,256]{1,0:T(8,128)(2,1)S(1)} fusion(bf16[1025,256]{1,0:T(8,128)(2,1)S(1)} %concatenate.6, s32[2048]{0:T(1024)S(1)} %get-tuple-element.6), kind=kCustom, calls=%fused_computation | custom fusion | bytes 2105344 | tf_op jit(solution)/shard_map/gather | solution.py:57
  31.6 24.1 %all_to_all.15 = bf16[16,2,64,256]{3,2,1,0:T(8,128)(2,1)S(1)} all-to-all(bf16[16,2,64,256]{3,2,1,0:T(8,128)(2,1)S(1)} %bitcast.52), channel_id=1, replica_groups=mesh['expert'=16,'mp'=8] {'expert'}, dimensions={0} | all-to-all | bytes 2097152 | tf_op jit(solution)/shard_map/all_to_all | solution.py:60
  55.7 1.1 copy.21
  56.9 9.5 %gather_fusion.2 = bf16[2048,896]{1,0:T(8,128)(2,1)} fusion(bf16[129,896]{1,0:T(8,128)(2,1)S(1)} %concatenate.7, s32[2048]{0:T(1024)S(1)} %get-tuple-element.5), kind=kCustom, calls=%fused_computation.2 | custom fusion | bytes 7348224 | tf_op jit(solution)/shard_map/gather | solution.py:45
  66.3 4.5 %all-to-all-start.2 = ((bf16[16,2,64,896]{3,2,1,0:T(8,128)(2,1)}), bf16[16,2,64,896]{3,2,1,0:T(8,128)(2,1)}, u32[]{:S(2)}, u32[]{:S(2)}) async-start(bf16[16,2,64,896]{3,2,1,0:T(8,128)(2,1)} %bitcast.50), calls=%async_computation.2 | async-start | bytes 7340032 | tf_op jit(solution)/shard_map/all_to_all | solution.py:59
  70.9 13.1 %all_gather.6 = f32[2,2048]{1,0:T(2,128)S(1)} all-gather(f32[2,256]{1,0:T(2,128)S(1)} %copy-done.1), channel_id=1, replica_groups=mesh['expert'=16,'mp'=8] {'mp'}, dimensions={1}, use_global_device_ids=true | all-gather | bytes 18432 | tf_op jit(solution)/shard_map/all_gather | solution.py:46
  84.0 25.2 %all-gather.2.cloned.1.call-done = bf16[16,2,64,2048]{3,2,0,1:T(8,128)(2,1)} async-done(((bf16[16,2,64,256]{3,2,0,1:T(8,128)(2,1)}), bf16[16,2,64,2048]{3,2,0,1:T(8,128)(2,1)}) %all-gather.2.cloned.1.call-update) | async-done | bytes 8388624 | tf_op jit(solution)/shard_map/all_gather | solution.py:62
  109.1 64.9 %convert_bitcast_fusion = bf16[16,2,64,896]{3,2,0,1:T(8,128)(2,1)S(1)} fusion(bf16[16,2,64,2048]{3,2,0,1:T(8,128)(2,1)} %all-gather.2.cloned.1.call-done, f32[2,2048]{1,0:T(2,128)S(1)} %all_gather.6, bf16[2,896,2048]{2,1,0:T(8,128)(2,1)} %param.7), kind=kOutput, calls=%fused_computation.22 | convolution fusion | flops 7551057920 | bytes 19415040 | tf_op jit(solution)/shard_map/sjcf,jdf->sjcd/dot_general | solution.py:70
  174.0 2.2 copy.22
  176.3 6.9 %all-to-all-start.1 = ((bf16[16,2,64,896]{3,2,1,0:T(8,128)(2,1)}), bf16[16,2,64,896]{3,2,1,0:T(8,128)(2,1)}, u32[]{:S(2)}, u32[]{:S(2)}) async-start(bf16[16,2,64,896]{3,2,1,0:T(8,128)(2,1)} %copy.22), calls=%async_computation.1 | async-start | bytes 7340032 | tf_op jit(solution)/shard_map/all_to_all | solution.py:73
  183.1 0.2 reduce-scatter.4.cloned.1.call-start
  183.4 70.7 %fusion.1 = (f32[2,2048]{1,0:T(2,128)S(1)}, bf16[2,896,2048]{2,1,0:T(8,128)(2,1)}) fusion(f32[2,2048]{1,0:T(2,128)S(1)} %all_gather.6, bf16[2,896,2048]{2,1,0:T(8,128)(2,1)} %param.7, bf16[16,2,64,896]{3,2,1,0:T(8,128)(2,1)} %all-to-all-done.2, bf16[16,2,64,2048]{3,2,0,1:T(8,128)(2,1)} %all-gather.2.cloned.1.call-done), kind=kOutput, calls=%fused_computation.7 | convolution fusion | flops 7582248960 | bytes 26771456 | tf_op jit(solution)/shard_map/sjcd,sjcf->jdf/dot_general | solution.py:63
  254.0 1.4 copy.27
  255.5 33.8 %reduce-scatter.4.cloned.1.call-done = f32[256,2]{1,0:T(8,128)} async-done(((f32[2048,2]{1,0:T(8,128)}), f32[256,2]{1,0:T(8,128)}) %reduce-scatter.4.cloned.1.call-update) | async-done | bytes 2064
  289.3 1.0 copy.28
  290.3 0.6 broadcast_multiply_fusion.1
  290.9 7.2 %gather_fusion.1 = bf16[1024,896]{1,0:T(8,128)(2,1)S(1)} fusion(bf16[2048,896]{1,0:T(8,128)(2,1)} %bitcast.9, s32[1024]{0:T(1024)S(1)} %broadcast_clamp_fusion), kind=kCustom, calls=%fused_computation.1 | custom fusion | bytes 3674112 | tf_op jit(solution)/shard_map/gather | solution.py:74
  298.0 1.9 bitcast_reduce_fusion
  (25 shorter events, 0.9 us)
Async XLA Ops:
  7.2 101.9 %all-gather.2.cloned.1.call-start = ((), (), s32[]{:S(2)}) async-start(), calls=%async_computation.4 | async-start | bytes 9437184 | tf_op jit(solution)/shard_map/all_gather | solution.py:62
  17.9 38.9 %copy-start = (bf16[128,896]{1,0:T(8,128)(2,1)S(1)}, bf16[128,896]{1,0:T(8,128)(2,1)}, u32[]{:S(2)}) copy-start(bf16[128,896]{1,0:T(8,128)(2,1)} %param.5) | copy-start | bytes 688132
  56.9 14.0 %copy-start.1 = (f32[2,256]{1,0:T(2,128)S(1)}, f32[2,256]{1,0:T(2,128)}, u32[]{:S(2)}) copy-start(f32[2,256]{1,0:T(2,128)} %param.8) | copy-start | bytes 6148
  66.3 109.9 %all-to-all-start.2 = ((bf16[16,2,64,896]{3,2,1,0:T(8,128)(2,1)}), bf16[16,2,64,896]{3,2,1,0:T(8,128)(2,1)}, u32[]{:S(2)}, u32[]{:S(2)}) async-start(bf16[16,2,64,896]{3,2,1,0:T(8,128)(2,1)} %bitcast.50), calls=%async_computation.2 | async-start | bytes 7340032 | tf_op jit(solution)/shard_map/all_to_all | solution.py:59
  176.3 114.6 %all-to-all-start.1 = ((bf16[16,2,64,896]{3,2,1,0:T(8,128)(2,1)}), bf16[16,2,64,896]{3,2,1,0:T(8,128)(2,1)}, u32[]{:S(2)}, u32[]{:S(2)}) async-start(bf16[16,2,64,896]{3,2,1,0:T(8,128)(2,1)} %copy.22), calls=%async_computation.1 | async-start | bytes 7340032 | tf_op jit(solution)/shard_map/all_to_all | solution.py:73
  183.1 106.1 %reduce-scatter.4.cloned.1.call-start = ((), (), s32[]{:S(2)}) async-start(), calls=%async_computation.5 | async-start | bytes 1179648
Sparse Core Ops, SparseCore 0:
  57.0 52.1 all-gather.1
  255.6 33.6 reduce-scatter.3
where the time goes:
time: 307 us
  matrix products  136 us (44%)
  waiting for transfers between devices  59 us (19%)
  blocking collectives  37.2 us (12%)
  local copies, waits for them, and re-layouts  36.7 us (12%)
  between operations  14.2 us (5%)
  other arithmetic  12.4 us (4%)
  starting transfers between devices  11.7 us (4%)
    dot_general x1, matrix products, per_device(): jnp.einsum('sjcd,sjcf->jdf', x_recv, g_recv, preferred_element_type=jnp.f...  70.7 us
    dot_general x1, matrix products, per_device(): jnp.einsum('sjcf,jdf->sjcd', g_recv, quantized, preferred_element_type=jn...  64.9 us
    unnamed x3, waiting for transfers between devices  33.9 us
    all_gather x1, waiting for transfers between devices, per_device(): g_recv = lax.all_gather(g_part, 'mp', axis=3, tiled=True)  25.2 us
    all_to_all x1, blocking collectives, per_device(): lax.all_to_all(g_slots, 'expert', split_axis=0, concat_axis=0, tiled=True)  24.1 us
    all_gather x1, blocking collectives, per_device(): full_steps = lax.all_gather(steps, 'mp', axis=1, tiled=True)  13.1 us
    gather x1, local copies, waits for them, and re-layouts, per_device(): padded_x[token_of].reshape(groups, local_experts, capacity, width_part)  9.47 us
    another operation x3, other arithmetic  9.15 us
  transfers between devices with their start and end apart: 4, of which 2 were waited for; matrix products, arithmetic and copies ran while one was open for 49% of the time, Pallas kernels for 0%

commit v1 on v0

--- a/solution.py
+++ b/solution.py
@@ -59,7 +59,11 @@
         lax.all_to_all(x_slots, "expert", split_axis=0, concat_axis=0, tiled=True),
         lax.all_to_all(g_slots, "expert", split_axis=0, concat_axis=0, tiled=True),
     )
-    g_recv = lax.all_gather(g_part, "mp", axis=3, tiled=True)
+    peers = lax.axis_size("mp")
+    repeats = [peers if d == 3 else 1 for d in range(g_part.ndim)]
+    g_recv = lax.all_to_all(
+        jnp.tile(g_part, repeats), "mp", split_axis=3, concat_axis=3, tiled=True
+    )
     raw = jnp.einsum("sjcd,sjcf->jdf", x_recv, g_recv, preferred_element_type=jnp.float32)
     weight_out = (raw * slopes).astype(jnp.bfloat16)
     full_width = width_part * lax.axis_size("mp")

time: 307 us -> 444 us (1.45)
  blocking collectives: 37.2 us -> 114 us
  other arithmetic: 12.4 us -> 66.8 us
  local copies, waits for them, and re-layouts: 36.7 us -> 80.1 us
  matrix products: 136 us -> 101 us
  waiting for transfers between devices: 59 us -> 51.7 us
    all_gather x1, blocking collectives: 13.1 us -> 89.7 us  [per_device(): full_steps = lax.all_gather(steps, 'mp', axis=1, tiled=True)]
    dot_general x0 -> x1, other arithmetic: none -> 54.3 us  [per_device(): jnp.einsum('sjcf,jdf->sjcd', g_recv, quantized, preferred_element_type=jn...]
    dot_general x1, matrix products: 64.9 us -> 17.7 us  [per_device(): jnp.einsum('sjcf,jdf->sjcd', g_recv, quantized, preferred_element_type=jn...]
    unnamed x7 -> x9, local copies, waits for them, and re-layouts: 3.14 us -> 36.5 us
    all_gather x1 -> x0, waiting for transfers between devices: 25.2 us -> none  [per_device(): g_recv = lax.all_gather(g_part, 'mp', axis=3, tiled=True)]
    all_to_all x1, waiting for transfers between devices: 0.01 us -> 18.5 us  [per_device(): lax.all_to_all(x_slots, 'expert', split_axis=0, concat_axis=0, tiled=True)]
    dot_general x1, matrix products: 70.7 us -> 83.4 us  [per_device(): jnp.einsum('sjcd,sjcf->jdf', x_recv, g_recv, preferred_element_type=jnp.f...]
    another operation x2 -> x3, local copies, waits for them, and re-layouts: 0.08 us -> 6.18 us  [the longest x1 6.1 us: per_device(): jnp.tile(g_part, repeats)]
  transfers between devices with their start and end apart: 4 -> 4, of which waited for: 2 -> 2; matrix products, arithmetic and copies ran while one was open for 49% -> 43% of each run, Pallas kernels for 0% -> 0%
where the time goes in v1:
time: 444 us; the launch traced here: 443 us
  blocking collectives  114 us (26%)
  matrix products  101 us (23%)
  local copies, waits for them, and re-layouts  80.1 us (18%)
  other arithmetic  66.8 us (15%)
  waiting for transfers between devices  51.7 us (12%)
  starting transfers between devices  14.9 us (3%)
  between operations  14.2 us (3%)
    all_gather x1, blocking collectives, per_device(): full_steps = lax.all_gather(steps, 'mp', axis=1, tiled=True)  89.7 us
    dot_general x1, matrix products, per_device(): jnp.einsum('sjcd,sjcf->jdf', x_recv, g_recv, preferred_element_type=jnp.f...  83.4 us
    dot_general x1, other arithmetic, per_device(): jnp.einsum('sjcf,jdf->sjcd', g_recv, quantized, preferred_element_type=jn...  54.3 us
    unnamed x9, local copies, waits for them, and re-layouts  36.5 us
    unnamed x2, waiting for transfers between devices  33.2 us
    all_to_all x1, blocking collectives, per_device(): lax.all_to_all(g_slots, 'expert', split_axis=0, concat_axis=0, tiled=True)  24.1 us
    all_to_all x1, waiting for transfers between devices, per_device(): lax.all_to_all(x_slots, 'expert', split_axis=0, concat_axis=0, tiled=True)  18.5 us
    dot_general x1, matrix products, per_device(): jnp.einsum('sjcf,jdf->sjcd', g_recv, quantized, preferred_element_type=jn...  17.7 us
  transfers between devices with their start and end apart: 4, of which 2 were waited for; matrix products, arithmetic and copies ran while one was open for 43% of the time, Pallas kernels for 0%

profile of v1, /device:TPU:0, one launch (start us, length us, event | category | flops | bytes accessed | tf_op | source)
XLA Modules:
  0.0 442.5 jit_solution(7369058231346680314)
XLA Ops:
  9.0 9.0 %reduce-window.6 = s32[32,8,128]{2,1,0:T(8,128)S(1)} reduce-window(s32[32,8,128]{2,1,0:T(8,128)S(1)} %fusion.20, s32[]{:T(128)} %constant.43.clone.1), window={size=1x1x128 pad=0_0x0_0x127_0}, to_apply=%region_0.0 | reduce-window | flops 4161536 | bytes 262148 | tf_op jit(solution)/shard_map/reduce-window
  18.6 4.3 scatter_custom_fusion
  22.9 1.1 concatenate.6
  24.0 7.5 %gather_fusion = bf16[2048,256]{1,0:T(8,128)(2,1)S(1)} fusion(bf16[1025,256]{1,0:T(8,128)(2,1)S(1)} %concatenate.6, s32[2048]{0:T(1024)S(1)} %get-tuple-element.6), kind=kCustom, calls=%fused_computation | custom fusion | bytes 2105344 | tf_op jit(solution)/shard_map/gather | solution.py:57
  31.5 24.1 %all_to_all.20 = bf16[16,2,64,256]{3,2,1,0:T(8,128)(2,1)S(1)} all-to-all(bf16[16,2,64,256]{3,2,1,0:T(8,128)(2,1)S(1)} %bitcast.58), channel_id=1, replica_groups=mesh['expert'=16,'mp'=8] {'expert'}, dimensions={0} | all-to-all | bytes 2097152 | tf_op jit(solution)/shard_map/all_to_all | solution.py:60
  55.6 3.1 copy.22
  58.7 6.1 %tile.4 = bf16[16,2,64,8,256]{2,0,1,4,3:T(8,128)(2,1)} broadcast(bf16[16,2,64,256]{2,0,1,3:T(8,128)(2,1)S(1)} %copy.22), dimensions={0,1,2,4} | broadcast | bytes 9437184 | tf_op jit(solution)/shard_map/tile | solution.py:65
  64.8 16.9 %reshape.118 = bf16[8,2,262144]{2,1,0:T(2,128)(2,1)} reshape(bf16[2048,2,16,64]{3,2,1,0:T(8,128)(2,1)} %bitcast.53) | data formatting | bytes 16777216
  81.7 5.3 %all-to-all-start.1 = ((bf16[8,2,262144]{2,1,0:T(2,128)(2,1)}), bf16[8,2,262144]{2,1,0:T(2,128)(2,1)}, u32[]{:S(2)}, u32[]{:S(2)}) async-start(bf16[8,2,262144]{2,1,0:T(2,128)(2,1)} %reshape.118), calls=%async_computation.1 | async-start | bytes 16777216 | tf_op jit(solution)/shard_map/all_to_all | solution.py:64
  87.0 9.5 %gather_fusion.2 = bf16[2048,896]{1,0:T(8,128)(2,1)} fusion(bf16[129,896]{1,0:T(8,128)(2,1)S(1)} %concatenate.7, s32[2048]{0:T(1024)S(1)} %get-tuple-element.5), kind=kCustom, calls=%fused_computation.2 | custom fusion | bytes 7348224 | tf_op jit(solution)/shard_map/gather | solution.py:45
  96.5 89.7 %all_gather.3 = f32[2,2048]{1,0:T(2,128)S(1)} all-gather(f32[2,256]{1,0:T(2,128)S(1)} %copy-done.1), channel_id=1, replica_groups=mesh['expert'=16,'mp'=8] {'mp'}, dimensions={1}, use_global_device_ids=true | all-gather | bytes 18432 | tf_op jit(solution)/shard_map/all_gather | solution.py:46
  186.2 54.3 %fusion.35 = bf16[2,896,2048,1]{2,1,3,0:T(8,128)(2,1)} fusion(f32[2,2048]{1,0:T(2,128)S(1)} %all_gather.3, bf16[2,896,2048]{2,1,0:T(8,128)(2,1)} %param.7), kind=kLoop, calls=%fused_computation.17.clone.clone.clone.clone.1 | loop fusion | flops 33030144 | bytes 14696448 | tf_op jit(solution)/shard_map/sjcf,jdf->sjcd/dot_general | solution.py:74
  240.6 4.7 %all-to-all-start.3 = ((bf16[16,2,64,896]{3,2,1,0:T(8,128)(2,1)}), bf16[16,2,64,896]{3,2,1,0:T(8,128)(2,1)}, u32[]{:S(2)}, u32[]{:S(2)}) async-start(bf16[16,2,64,896]{3,2,1,0:T(8,128)(2,1)} %bitcast.56), calls=%async_computation.3 | async-start | bytes 7340032 | tf_op jit(solution)/shard_map/all_to_all | solution.py:59
  245.3 16.5 %reshape.119 = bf16[2048,2,16,64]{3,2,1,0:T(8,128)(2,1)} reshape(bf16[8,2,262144]{2,1,0:T(2,128)(2,1)} %all-to-all-done.1) | data formatting | bytes 16777216
  261.8 17.7 %convert_bitcast_fusion = bf16[16,2,64,896]{3,2,0,1:T(8,128)(2,1)} fusion(bf16[16,2,64,2048]{2,0,1,3:T(8,128)(2,1)} %bitcast.54, bf16[2,896,2048,1]{2,1,3,0:T(8,128)(2,1)} %fusion.35), kind=kOutput, calls=%fused_computation.23 | convolution fusion | flops 7518027776 | bytes 19398656 | tf_op jit(solution)/shard_map/sjcf,jdf->sjcd/dot_general | solution.py:74
  279.5 4.2 copy.24
  283.7 18.5 %all-to-all-done.3 = bf16[16,2,64,896]{3,2,1,0:T(8,128)(2,1)} async-done(((bf16[16,2,64,896]{3,2,1,0:T(8,128)(2,1)}), bf16[16,2,64,896]{3,2,1,0:T(8,128)(2,1)}, u32[]{:S(2)}, u32[]{:S(2)}) %all-to-all-start.3) | async-done | bytes 3670048 | tf_op jit(solution)/shard_map/all_to_all | solution.py:59
  302.2 4.6 %all-to-all-start.2 = ((bf16[16,2,64,896]{3,2,1,0:T(8,128)(2,1)}), bf16[16,2,64,896]{3,2,1,0:T(8,128)(2,1)}, u32[]{:S(2)}, u32[]{:S(2)}) async-start(bf16[16,2,64,896]{3,2,1,0:T(8,128)(2,1)} %copy.24), calls=%async_computation.2 | async-start | bytes 7340032 | tf_op jit(solution)/shard_map/all_to_all | solution.py:77
  307.1 83.4 %fusion.5 = (f32[2,2048]{1,0:T(2,128)S(1)}, bf16[2,896,2048]{2,1,0:T(8,128)(2,1)}) fusion(f32[2,2048]{1,0:T(2,128)S(1)} %all_gather.3, bf16[2,896,2048]{2,1,0:T(8,128)(2,1)} %param.7, bf16[16,2,64,896]{3,2,1,0:T(8,128)(2,1)} %all-to-all-done.3, bf16[16,2,64,2048]{2,0,1,3:T(8,128)(2,1)} %bitcast.55), kind=kOutput, calls=%fused_computation.11 | convolution fusion | flops 7582248960 | bytes 26771456 | tf_op jit(solution)/shard_map/sjcd,sjcf->jdf/dot_general | solution.py:67
  390.5 1.3 copy.31
  391.8 33.2 %reduce-scatter.4.cloned.1.call-done = f32[256,2]{1,0:T(8,128)} async-done(((f32[2048,2]{1,0:T(8,128)}), f32[256,2]{1,0:T(8,128)}) %reduce-scatter.4.cloned.1.call-update) | async-done | bytes 2064
  425.0 1.0 copy.32
  426.6 7.2 %gather_fusion.1 = bf16[1024,896]{1,0:T(8,128)(2,1)S(1)} fusion(bf16[2048,896]{1,0:T(8,128)(2,1)} %bitcast.10, s32[1024]{0:T(1024)S(1)} %broadcast_clamp_fusion), kind=kCustom, calls=%fused_computation.1 | custom fusion | bytes 3674112 | tf_op jit(solution)/shard_map/gather | solution.py:78
  433.8 1.9 bitcast_reduce_fusion
  (28 shorter events, 3.3 us)
Async XLA Ops:
  64.8 22.2 %copy-start = (bf16[128,896]{1,0:T(8,128)(2,1)S(1)}, bf16[128,896]{1,0:T(8,128)(2,1)}, u32[]{:S(2)}) copy-start(bf16[128,896]{1,0:T(8,128)(2,1)} %param.5) | copy-start | bytes 688132
  81.7 158.9 %all-to-all-start.1 = ((bf16[8,2,262144]{2,1,0:T(2,128)(2,1)}), bf16[8,2,262144]{2,1,0:T(2,128)(2,1)}, u32[]{:S(2)}, u32[]{:S(2)}) async-start(bf16[8,2,262144]{2,1,0:T(2,128)(2,1)} %reshape.118), calls=%async_computation.1 | async-start | bytes 16777216 | tf_op jit(solution)/shard_map/all_to_all | solution.py:64
  87.0 9.5 %copy-start.1 = (f32[2,256]{1,0:T(2,128)S(1)}, f32[2,256]{1,0:T(2,128)}, u32[]{:S(2)}) copy-start(f32[2,256]{1,0:T(2,128)} %param.8) | copy-start | bytes 6148
  240.6 61.6 %all-to-all-start.3 = ((bf16[16,2,64,896]{3,2,1,0:T(8,128)(2,1)}), bf16[16,2,64,896]{3,2,1,0:T(8,128)(2,1)}, u32[]{:S(2)}, u32[]{:S(2)}) async-start(bf16[16,2,64,896]{3,2,1,0:T(8,128)(2,1)} %bitcast.56), calls=%async_computation.3 | async-start | bytes 7340032 | tf_op jit(solution)/shard_map/all_to_all | solution.py:59
  302.2 124.4 %all-to-all-start.2 = ((bf16[16,2,64,896]{3,2,1,0:T(8,128)(2,1)}), bf16[16,2,64,896]{3,2,1,0:T(8,128)(2,1)}, u32[]{:S(2)}, u32[]{:S(2)}) async-start(bf16[16,2,64,896]{3,2,1,0:T(8,128)(2,1)} %copy.24), calls=%async_computation.2 | async-start | bytes 7340032 | tf_op jit(solution)/shard_map/all_to_all | solution.py:77
  306.8 118.2 %reduce-scatter.4.cloned.1.call-start = ((), (), s32[]{:S(2)}) async-start(), calls=%async_computation.5 | async-start | bytes 1179648
Sparse Core Ops, SparseCore 0:
  391.9 33.0 reduce-scatter.3
